TPU v7x, 8 devices: a whole 2x2x1 slice. The times are simulated.
8 devices in a mesh: pp: 2 (over z, y), dp: 4 (over x, core).
Axes of the slice: x: 2, y: 2, z: 1, core: 2. Of those that a mesh axis runs over, the one named last changes fastest.
Arguments:
- act_in: bfloat16 [4, 12, 384, 1536], P(None, 'dp')
- loss_seed: bfloat16 [4, 12, 384, 1536], P(None, 'dp')
- w_qkv: bfloat16 [2, 1536, 48, 96], P('pp', 'dp')
- w_proj: bfloat16 [2, 1536, 1536], P('pp', 'dp')
- w_up: bfloat16 [2, 1536, 6144], P('pp', 'dp')
- w_down: bfloat16 [2, 6144, 1536], P('pp', 'dp')
Outputs:
- output 1: float32 [2, 1536, 48, 96], P('pp', 'dp')
- output 2: float32 [2, 1536, 1536], P('pp', 'dp')
- output 3: float32 [2, 1536, 6144], P('pp', 'dp')
- output 4: float32 [2, 6144, 1536], P('pp', 'dp')
- output 5: bfloat16 [4, 12, 384, 1536], P(None, 'dp', 'pp')
All inputs are finite; a program needn't handle non-finite values.
Results may differ from a plain program's by a relative error of at most 0.0197363.
Values are sent between devices in bfloat16 or wider.
A program may use at most 1 GiB of HBM per device.

v0:
```python
import jax
import jax.numpy as jnp
from jax import lax
from jax.sharding import PartitionSpec as P

NORM_EPS = 1e-6


def rms_norm(hidden):
    return hidden * lax.rsqrt(jnp.mean(hidden * hidden, axis=-1, keepdims=True) + NORM_EPS)


def gelu_tanh(pre_act):
    return jax.nn.gelu(pre_act, approximate=True)


def attn_core(q_heads, k_heads, v_heads):
    seq_len = q_heads.shape[1]
    scores = jnp.einsum('bqnh,bknh->bnqk', q_heads, k_heads, preferred_element_type=jnp.float32) * (q_heads.shape[-1] ** -0.5)
    causal = jnp.arange(seq_len)[:, None] >= jnp.arange(seq_len)[None, :]
    prob_bf = jax.nn.softmax(jnp.where(causal, scores, -1e30), axis=-1).astype(jnp.bfloat16)
    return jnp.einsum('bnqk,bknh->bqnh', prob_bf, v_heads, preferred_element_type=jnp.float32).astype(jnp.bfloat16)


def layer_forward(hidden, w_qkv, w_proj, w_up, w_down):
    num_heads = w_qkv.shape[1] // 3
    hid_f32 = hidden.astype(jnp.float32)
    normed = rms_norm(hid_f32).astype(jnp.bfloat16)
    qkv_act = jnp.einsum('bsd,dnh->bsnh', normed, w_qkv, preferred_element_type=jnp.float32).astype(jnp.bfloat16)
    q_heads = qkv_act[:, :, :num_heads]
    k_heads = qkv_act[:, :, num_heads:2 * num_heads]
    v_heads = qkv_act[:, :, 2 * num_heads:]
    attn_flat = attn_core(q_heads, k_heads, v_heads).reshape(hidden.shape)
    mid_f32 = (hid_f32 + jnp.einsum('bse,ed->bsd', attn_flat, w_proj, preferred_element_type=jnp.float32)).astype(jnp.bfloat16).astype(jnp.float32)
    normed2 = rms_norm(mid_f32).astype(jnp.bfloat16)
    up_act = jnp.einsum('bsd,df->bsf', normed2, w_up, preferred_element_type=jnp.float32).astype(jnp.bfloat16)
    gelu_out = gelu_tanh(up_act.astype(jnp.float32)).astype(jnp.bfloat16)
    block_out = (mid_f32 + jnp.einsum('bsf,fd->bsd', gelu_out, w_down, preferred_element_type=jnp.float32)).astype(jnp.bfloat16)
    saved_acts = (hid_f32, normed, q_heads, k_heads, v_heads, attn_flat, mid_f32, normed2, up_act, gelu_out)
    return block_out, saved_acts


def layer_backward(saved_acts, ct_out, w_qkv, w_proj, w_up, w_down):
    hid_f32, normed, q_heads, k_heads, v_heads, attn_flat, mid_f32, normed2, up_act, gelu_out = saved_acts
    g_down = jnp.einsum('bsf,bsd->fd', gelu_out, ct_out, preferred_element_type=jnp.float32)
    ct_gelu = jnp.einsum('bsd,fd->bsf', ct_out, w_down, preferred_element_type=jnp.float32).astype(jnp.bfloat16)
    gelu_pull = jax.vjp(gelu_tanh, up_act.astype(jnp.float32))[1]
    ct_up = gelu_pull(ct_gelu.astype(jnp.float32))[0].astype(jnp.bfloat16)
    g_up = jnp.einsum('bsd,bsf->df', normed2, ct_up, preferred_element_type=jnp.float32)
    ct_norm2 = jnp.einsum('bsf,df->bsd', ct_up, w_up, preferred_element_type=jnp.float32).astype(jnp.bfloat16)
    norm_pull2 = jax.vjp(rms_norm, mid_f32)[1]
    ct_mid = (ct_out.astype(jnp.float32) + norm_pull2(ct_norm2.astype(jnp.float32))[0]).astype(jnp.bfloat16)
    g_proj = jnp.einsum('bse,bsd->ed', attn_flat, ct_mid, preferred_element_type=jnp.float32)
    ct_attn = jnp.einsum('bsd,ed->bse', ct_mid, w_proj, preferred_element_type=jnp.float32).astype(jnp.bfloat16)
    attn_pull = jax.vjp(attn_core, q_heads, k_heads, v_heads)[1]
    ct_q, ct_k, ct_v = attn_pull(ct_attn.reshape(q_heads.shape))
    ct_qkv = jnp.concatenate([ct_q, ct_k, ct_v], axis=2)
    g_qkv = jnp.einsum('bsd,bsnh->dnh', normed, ct_qkv, preferred_element_type=jnp.float32)
    ct_norm = jnp.einsum('bsnh,dnh->bsd', ct_qkv, w_qkv, preferred_element_type=jnp.float32).astype(jnp.bfloat16)
    norm_pull = jax.vjp(rms_norm, hid_f32)[1]
    ct_hidden = (ct_mid.astype(jnp.float32) + norm_pull(ct_norm.astype(jnp.float32))[0]).astype(jnp.bfloat16)
    return ct_hidden, (g_qkv, g_proj, g_up, g_down)


def stage_forward(hidden, weights):
    for layer_idx in range(weights[0].shape[0]):
        hidden = layer_forward(hidden, weights[0][layer_idx], weights[1][layer_idx], weights[2][layer_idx], weights[3][layer_idx])[0]
    return hidden


def stage_backward(hidden, ct_out, weights):
    num_layers = weights[0].shape[0]
    saved_list = []
    for layer_idx in range(num_layers):
        layer_w = tuple(w_full[layer_idx] for w_full in weights)
        hidden, saved_acts = layer_forward(hidden, *layer_w)
        saved_list.append(saved_acts)
    grad_lists = ([], [], [], [])
    for layer_idx in reversed(range(num_layers)):
        layer_w = tuple(w_full[layer_idx] for w_full in weights)
        ct_out, layer_grads = layer_backward(saved_list[layer_idx], ct_out, *layer_w)
        for grad_list, grad_part in zip(grad_lists, layer_grads):
            grad_list.append(grad_part)
    return ct_out, tuple(jnp.stack(grad_list[::-1]) for grad_list in grad_lists)


def solution(mesh):
    stages = mesh.shape['pp']
    fwd_pairs = [(src_idx, src_idx + 1) for src_idx in range(stages - 1)]
    bwd_pairs = [(src_idx + 1, src_idx) for src_idx in range(stages - 1)]

    def device_step(act_in, loss_seed, w_qkv, w_proj, w_up, w_down):
        num_micro = act_in.shape[0]
        num_ticks = num_micro + 2 * stages - 2
        stage_idx = lax.axis_index('pp')
        weights = tuple(lax.all_gather(w_part, 'dp', axis=1, tiled=True) for w_part in (w_qkv, w_proj, w_up, w_down))
        zero_act = jnp.zeros(act_in.shape[1:], jnp.bfloat16)
        grad_init = tuple(jnp.zeros(w_full.shape, jnp.float32) for w_full in weights)

        def run_forward(hidden):
            return stage_forward(hidden, weights)

        def run_backward(hidden, ct_out, grad_acc):
            ct_in, stage_grads = stage_backward(hidden, ct_out, weights)
            return ct_in, tuple(acc_part + grad_part for acc_part, grad_part in zip(grad_acc, stage_grads))

        def skip_backward(hidden, ct_out, grad_acc):
            return jnp.zeros_like(hidden), grad_acc

        def run_tick(tick_idx, loop_state):
            fwd_buf, bwd_buf, stash_in, outputs, grad_acc = loop_state
            fwd_idx = tick_idx - stage_idx
            fwd_ok = (fwd_idx >= 0) & (fwd_idx < num_micro)
            fwd_slot = jnp.clip(fwd_idx, 0, num_micro - 1)
            fresh_in = lax.dynamic_index_in_dim(act_in, fwd_slot, 0, keepdims=False)
            stage_in = jnp.where(stage_idx == 0, fresh_in, fwd_buf)
            stage_out = lax.cond(fwd_ok, run_forward, jnp.zeros_like, stage_in)
            old_in = lax.dynamic_index_in_dim(stash_in, fwd_slot, 0, keepdims=False)
            stash_in = lax.dynamic_update_index_in_dim(stash_in, jnp.where(fwd_ok, stage_in, old_in), fwd_slot, 0)
            old_out = lax.dynamic_index_in_dim(outputs, fwd_slot, 0, keepdims=False)
            outputs = lax.dynamic_update_index_in_dim(outputs, jnp.where(fwd_ok, stage_out, old_out), fwd_slot, 0)
            bwd_idx = tick_idx - (2 * stages - 2) + stage_idx
            bwd_ok = (bwd_idx >= 0) & (bwd_idx < num_micro)
            bwd_slot = jnp.clip(bwd_idx, 0, num_micro - 1)
            seed_now = lax.dynamic_index_in_dim(loss_seed, bwd_slot, 0, keepdims=False)
            ct_out = jnp.where(stage_idx == stages - 1, seed_now, bwd_buf)
            saved_in = lax.dynamic_index_in_dim(stash_in, bwd_slot, 0, keepdims=False)
            ct_in, grad_acc = lax.cond(bwd_ok, run_backward, skip_backward, saved_in, ct_out, grad_acc)
            fwd_buf = lax.ppermute(stage_out, 'pp', fwd_pairs)
            bwd_buf = lax.ppermute(ct_in, 'pp', bwd_pairs)
            return fwd_buf, bwd_buf, stash_in, outputs, grad_acc

        loop_init = (zero_act, zero_act, jnp.zeros_like(act_in), jnp.zeros_like(act_in), grad_init)
        loop_state = lax.fori_loop(0, num_ticks, run_tick, loop_init)
        outputs, grad_acc = loop_state[3], loop_state[4]
        grad_shards = tuple(lax.psum_scatter(acc_part, 'dp', scatter_dimension=1, tiled=True) for acc_part in grad_acc)
        last_out = jnp.where(stage_idx == stages - 1, outputs, jnp.zeros_like(outputs))
        out_shard = lax.psum_scatter(last_out, 'pp', scatter_dimension=2, tiled=True)
        return grad_shards + (out_shard,)

    weight_spec = P('pp', 'dp')
    act_spec = P(None, 'dp')
    return jax.shard_map(device_step, mesh=mesh, in_specs=(act_spec, act_spec, weight_spec, weight_spec, weight_spec, weight_spec), out_specs=(weight_spec, weight_spec, weight_spec, weight_spec, P(None, 'dp', 'pp')), check_vma=False)
```

profile of v0, /device:TPU:0, one launch (start us, length us, event | category | flops | bytes accessed | tf_op | source)
XLA Modules:
  0.0 5155.3 jit_solution(8452785686178378318)
XLA Ops:
  10.0 36.9 all-gather.7.cloned.1.call-done
  46.9 90.4 %all-gather.5.cloned.1.call-done = bf16[1,1536,48,96]{1,3,2,0:T(8,128)(2,1)} async-done(((bf16[1,384,48,96]{1,3,2,0:T(8,128)(2,1)}), bf16[1,1536,48,96]{1,3,2,0:T(8,128)(2,1)}) %all-gather.5.cloned.1.call-update) | async-done | bytes 14155792 | tf_op jit(solution)/shard_map/all_gather | solution.py:96
  137.3 119.6 %all-gather.9.cloned.1.call-done = bf16[1,1536,6144]{2,1,0:T(8,128)(2,1)} async-done(((bf16[1,384,6144]{2,1,0:T(8,128)(2,1)}), bf16[1,1536,6144]{2,1,0:T(8,128)(2,1)}) %all-gather.9.cloned.1.call-update) | async-done | bytes 18874384 | tf_op jit(solution)/shard_map/all_gather | solution.py:96
  256.9 119.5 %all-gather.11.cloned.1.call-done = bf16[1,6144,1536]{2,1,0:T(8,128)(2,1)} async-done(((bf16[1,1536,1536]{2,1,0:T(8,128)(2,1)}), bf16[1,6144,1536]{2,1,0:T(8,128)(2,1)}) %all-gather.11.cloned.1.call-update) | async-done | bytes 18874384 | tf_op jit(solution)/shard_map/all_gather | solution.py:96
  435.8 3780.9 %while.29 = (s32[]{:T(128)}, bf16[3,384,1536]{2,1,0:T(8,128)(2,1)}, bf16[3,384,1536]{2,1,0:T(8,128)(2,1)}, bf16[4,3,384,1536]{3,2,1,0:T(8,128)(2,1)}, bf16[4,3,3...) while((s32[]{:T(128)}, bf16[3,384,1536]{2,1,0:T(8,128)(2,1)}, ...), condition=%wide.region_16.17_spmd, body=%wide.region_0.16_spmd.sunk | while | flops 250853097472 | bytes 1382539520 | solution.py:134
  443.6 175.1 %conditional.4 = (bf16[3,384,1536]{2,1,0:T(8,128)(2,1)}) conditional(s32[]{:T(128)} %convert_element_type.487, () %tuple.75, (bf16[3,384,1536]{2,1,0:T(8,128)(2,1)S(1)}, bf16[1,1536,48,96]{1,3,2,0:T(8,128)(2,1)}, bf16[1,1536,1536]{2,1,0:T(8,128)(2,1)}, bf16[1,1536,6144]{2,1,0:T(8,128)(2,1)}, bf16[1,6144,1536]{2,1,0:T(8,128)(2,1)}) %tuple.76), branch_computations={%region_1.1_spmd, %region_2.6_spmd} | conditional | flops 68156686336 | bytes 266047488 | solution.py:117
  554.8 32.8 fusion.207
  634.3 62.1 %collective-permute-done = bf16[3,384,1536]{2,1,0:T(8,128)(2,1)} collective-permute-done((bf16[3,384,1536]{2,1,0:T(8,128)(2,1)}, bf16[3,384,1536]{2,1,0:T(8,128)(2,1)}, u32[]{:S(2)}, u32[]{:S(2)}) %collective-permute-start) | collective-permute-done | bytes 3538976 | tf_op jit(solution)/shard_map/while/body/eval_jaxpr/ppermute | solution.py:129
  716.2 175.0 %conditional.4 = (bf16[3,384,1536]{2,1,0:T(8,128)(2,1)}) conditional(s32[]{:T(128)} %convert_element_type.487, () %tuple.75, (bf16[3,384,1536]{2,1,0:T(8,128)(2,1)S(1)}, bf16[1,1536,48,96]{1,3,2,0:T(8,128)(2,1)}, bf16[1,1536,1536]{2,1,0:T(8,128)(2,1)}, bf16[1,1536,6144]{2,1,0:T(8,128)(2,1)}, bf16[1,6144,1536]{2,1,0:T(8,128)(2,1)}) %tuple.76), branch_computations={%region_1.1_spmd, %region_2.6_spmd} | conditional | flops 68156686336 | bytes 266047488 | solution.py:117
  827.1 32.9 fusion.207
  912.0 57.2 %collective-permute-done = bf16[3,384,1536]{2,1,0:T(8,128)(2,1)} collective-permute-done((bf16[3,384,1536]{2,1,0:T(8,128)(2,1)}, bf16[3,384,1536]{2,1,0:T(8,128)(2,1)}, u32[]{:S(2)}, u32[]{:S(2)}) %collective-permute-start) | collective-permute-done | bytes 3538976 | tf_op jit(solution)/shard_map/while/body/eval_jaxpr/ppermute | solution.py:129
  969.1 469.2 %collective-permute-done.1 = bf16[3,384,1536]{2,1,0:T(8,128)(2,1)S(1)} collective-permute-done((bf16[3,384,1536]{2,1,0:T(8,128)(2,1)}, bf16[3,384,1536]{2,1,0:T(8,128)(2,1)S(1)}, u32[]{:S(2)}, u32[]{:S(2)}) %collective-permute-start.1) | collective-permute-done | bytes 3538976 | tf_op jit(solution)/shard_map/while/body/eval_jaxpr/ppermute | solution.py:130
  1448.0 175.0 %conditional.4 = (bf16[3,384,1536]{2,1,0:T(8,128)(2,1)}) conditional(s32[]{:T(128)} %convert_element_type.487, () %tuple.75, (bf16[3,384,1536]{2,1,0:T(8,128)(2,1)S(1)}, bf16[1,1536,48,96]{1,3,2,0:T(8,128)(2,1)}, bf16[1,1536,1536]{2,1,0:T(8,128)(2,1)}, bf16[1,1536,6144]{2,1,0:T(8,128)(2,1)}, bf16[1,6144,1536]{2,1,0:T(8,128)(2,1)}) %tuple.76), branch_computations={%region_1.1_spmd, %region_2.6_spmd} | conditional | flops 68156686336 | bytes 266047488 | solution.py:117
  1559.0 33.1 fusion.207
  1627.3 468.8 %conditional.5 = (bf16[3,384,1536]{2,1,0:T(8,128)(2,1)}, f32[1,1536,48,96]{1,3,2,0:T(8,128)}, f32[1,1536,1536]{2,1,0:T(8,128)}, f32[1,1536,6144]{2,1,0:T(8,128)}, f32[1,6144,1536]{2,1,0:T(8,128)}) conditional(s32[]{:T(128)} %convert_element_type.488, (f32[1,1536,48,96]{1,3,2,0:T(8,128)}, f32[1,1536,1536]{2,1,0:T(8,128)}, f32[1,1536,6144]{2,1,0:T(8,128)}, ...), branch_computations={%region_7.7_spmd, %region_8.15_spmd} | conditional | flops 182691102720 | bytes 1031556416 | solution.py:128
  1680.1 32.4 fusion.179
  1779.8 45.2 fusion.71
  1825.1 31.1 fusion.128
  2017.7 37.6 bitcast_add_fusion.1
  2055.3 40.3 bitcast_add_fusion
  2104.4 70.6 %collective-permute-done.1 = bf16[3,384,1536]{2,1,0:T(8,128)(2,1)S(1)} collective-permute-done((bf16[3,384,1536]{2,1,0:T(8,128)(2,1)}, bf16[3,384,1536]{2,1,0:T(8,128)(2,1)S(1)}, u32[]{:S(2)}, u32[]{:S(2)}) %collective-permute-start.1) | collective-permute-done | bytes 3538976 | tf_op jit(solution)/shard_map/while/body/eval_jaxpr/ppermute | solution.py:130
  2184.6 175.0 %conditional.4 = (bf16[3,384,1536]{2,1,0:T(8,128)(2,1)}) conditional(s32[]{:T(128)} %convert_element_type.487, () %tuple.75, (bf16[3,384,1536]{2,1,0:T(8,128)(2,1)S(1)}, bf16[1,1536,48,96]{1,3,2,0:T(8,128)(2,1)}, bf16[1,1536,1536]{2,1,0:T(8,128)(2,1)}, bf16[1,1536,6144]{2,1,0:T(8,128)(2,1)}, bf16[1,6144,1536]{2,1,0:T(8,128)(2,1)}) %tuple.76), branch_computations={%region_1.1_spmd, %region_2.6_spmd} | conditional | flops 68156686336 | bytes 266047488 | solution.py:117
  2295.5 32.9 fusion.207
  2363.9 468.7 %conditional.5 = (bf16[3,384,1536]{2,1,0:T(8,128)(2,1)}, f32[1,1536,48,96]{1,3,2,0:T(8,128)}, f32[1,1536,1536]{2,1,0:T(8,128)}, f32[1,1536,6144]{2,1,0:T(8,128)}, f32[1,6144,1536]{2,1,0:T(8,128)}) conditional(s32[]{:T(128)} %convert_element_type.488, (f32[1,1536,48,96]{1,3,2,0:T(8,128)}, f32[1,1536,1536]{2,1,0:T(8,128)}, f32[1,1536,6144]{2,1,0:T(8,128)}, ...), branch_computations={%region_7.7_spmd, %region_8.15_spmd} | conditional | flops 182691102720 | bytes 1031556416 | solution.py:128
  2416.7 32.4 fusion.179
  2516.4 45.2 fusion.71
  2754.3 37.6 bitcast_add_fusion.1
  2791.9 40.3 bitcast_add_fusion
  2840.9 69.5 %collective-permute-done.1 = bf16[3,384,1536]{2,1,0:T(8,128)(2,1)S(1)} collective-permute-done((bf16[3,384,1536]{2,1,0:T(8,128)(2,1)}, bf16[3,384,1536]{2,1,0:T(8,128)(2,1)S(1)}, u32[]{:S(2)}, u32[]{:S(2)}) %collective-permute-start.1) | collective-permute-done | bytes 3538976 | tf_op jit(solution)/shard_map/while/body/eval_jaxpr/ppermute | solution.py:130
  2931.1 168.2 %collective-permute-start = (bf16[3,384,1536]{2,1,0:T(8,128)(2,1)}, bf16[3,384,1536]{2,1,0:T(8,128)(2,1)}, u32[]{:S(2)}, u32[]{:S(2)}) collective-permute-start(bf16[3,384,1536]{2,1,0:T(8,128)(2,1)} %get-tuple-element.822), channel_id=1, source_target_pairs={{0,4},{1,5},{2,6},{3,7}} | collective-permute-start | bytes 10616840 | tf_op jit(solution)/shard_map/while/body/eval_jaxpr/ppermute | solution.py:129
  3099.3 468.4 %conditional.5 = (bf16[3,384,1536]{2,1,0:T(8,128)(2,1)}, f32[1,1536,48,96]{1,3,2,0:T(8,128)}, f32[1,1536,1536]{2,1,0:T(8,128)}, f32[1,1536,6144]{2,1,0:T(8,128)}, f32[1,6144,1536]{2,1,0:T(8,128)}) conditional(s32[]{:T(128)} %convert_element_type.488, (f32[1,1536,48,96]{1,3,2,0:T(8,128)}, f32[1,1536,1536]{2,1,0:T(8,128)}, f32[1,1536,6144]{2,1,0:T(8,128)}, ...), branch_computations={%region_7.7_spmd, %region_8.15_spmd} | conditional | flops 182691102720 | bytes 1031556416 | solution.py:128
  3152.0 32.1 fusion.179
  3251.5 45.3 fusion.71
  3296.8 31.3 fusion.128
  3489.6 37.6 bitcast_add_fusion.1
  3527.3 40.2 bitcast_add_fusion
  3574.0 70.3 %collective-permute-done.1 = bf16[3,384,1536]{2,1,0:T(8,128)(2,1)S(1)} collective-permute-done((bf16[3,384,1536]{2,1,0:T(8,128)(2,1)}, bf16[3,384,1536]{2,1,0:T(8,128)(2,1)S(1)}, u32[]{:S(2)}, u32[]{:S(2)}) %collective-permute-start.1) | collective-permute-done | bytes 3538976 | tf_op jit(solution)/shard_map/while/body/eval_jaxpr/ppermute | solution.py:130
  3669.3 468.8 %conditional.5 = (bf16[3,384,1536]{2,1,0:T(8,128)(2,1)}, f32[1,1536,48,96]{1,3,2,0:T(8,128)}, f32[1,1536,1536]{2,1,0:T(8,128)}, f32[1,1536,6144]{2,1,0:T(8,128)}, f32[1,6144,1536]{2,1,0:T(8,128)}) conditional(s32[]{:T(128)} %convert_element_type.488, (f32[1,1536,48,96]{1,3,2,0:T(8,128)}, f32[1,1536,1536]{2,1,0:T(8,128)}, f32[1,1536,6144]{2,1,0:T(8,128)}, ...), branch_computations={%region_7.7_spmd, %region_8.15_spmd} | conditional | flops 182691102720 | bytes 1031556416 | solution.py:128
  3722.1 32.4 fusion.179
  3821.8 45.2 fusion.71
  4059.7 37.6 bitcast_add_fusion.1
  4097.3 40.3 bitcast_add_fusion
  4144.4 69.2 %collective-permute-done.1 = bf16[3,384,1536]{2,1,0:T(8,128)(2,1)S(1)} collective-permute-done((bf16[3,384,1536]{2,1,0:T(8,128)(2,1)}, bf16[3,384,1536]{2,1,0:T(8,128)(2,1)S(1)}, u32[]{:S(2)}, u32[]{:S(2)}) %collective-permute-start.1) | collective-permute-done | bytes 3538976 | tf_op jit(solution)/shard_map/while/body/eval_jaxpr/ppermute | solution.py:130
  4224.8 62.4 %reduce-scatter.8.cloned.1.call-done = f32[1,384,1536]{2,1,0:T(8,128)} async-done(((f32[1,1536,1536]{2,1,0:T(8,128)}), f32[1,384,1536]{2,1,0:T(8,128)}) %reduce-scatter.8.cloned.1.call-update) | async-done | bytes 2359312 | tf_op jit(solution)/shard_map/reduce_scatter | solution.py:136
  4287.3 161.4 %reduce-scatter.14.cloned.1.call-done = bf16[4,3,192,1536]{3,2,1,0:T(8,128)(2,1)} async-done(((bf16[4,3,384,1536]{3,2,1,0:T(8,128)(2,1)}), bf16[4,3,192,1536]{3,2,1,0:T(8,128)(2,1)}) %reduce-scatter.14.cloned.1.call-update) | async-done | bytes 7077904 | tf_op jit(solution)/shard_map/reduce_scatter | solution.py:138
  4448.6 191.1 %reduce-scatter.6.cloned.1.call-done = f32[1,384,48,96]{1,3,2,0:T(8,128)} async-done(((f32[1,1536,48,96]{1,3,2,0:T(8,128)}), f32[1,384,48,96]{1,3,2,0:T(8,128)}) %reduce-scatter.6.cloned.1.call-update) | async-done | bytes 7077904 | tf_op jit(solution)/shard_map/reduce_scatter | solution.py:136
  4639.7 254.4 %reduce-scatter.10.cloned.1.call-done = f32[1,384,6144]{2,1,0:T(8,128)} async-done(((f32[1,1536,6144]{2,1,0:T(8,128)}), f32[1,384,6144]{2,1,0:T(8,128)}) %reduce-scatter.10.cloned.1.call-update) | async-done | bytes 9437200 | tf_op jit(solution)/shard_map/reduce_scatter | solution.py:136
  4894.1 254.4 %reduce-scatter.12.cloned.1.call-done = f32[1,1536,1536]{2,1,0:T(8,128)} async-done(((f32[1,6144,1536]{2,1,0:T(8,128)}), f32[1,1536,1536]{2,1,0:T(8,128)}) %reduce-scatter.12.cloned.1.call-update) | async-done | bytes 9437200 | tf_op jit(solution)/shard_map/reduce_scatter | solution.py:136
  (393 shorter events, 2001.6 us)
Async XLA Ops:
  7.2 39.7 all-gather.7.cloned.1.call-start
  7.9 129.4 %all-gather.5.cloned.1.call-start = ((), (), s32[]{:S(2)}) async-start(), calls=%async_computation.5 | async-start | bytes 17694720 | tf_op jit(solution)/shard_map/all_gather | solution.py:96
  8.6 248.3 %all-gather.9.cloned.1.call-start = ((), (), s32[]{:S(2)}) async-start(), calls=%async_computation.7 | async-start | bytes 23592960 | tf_op jit(solution)/shard_map/all_gather | solution.py:96
  9.4 367.0 %all-gather.11.cloned.1.call-start = ((), (), s32[]{:S(2)}) async-start(), calls=%async_computation.8 | async-start | bytes 23592960 | tf_op jit(solution)/shard_map/all_gather | solution.py:96
  10.0 4277.3 %reduce-scatter.8.cloned.1.call-start = ((), (), s32[]{:S(2)}) async-start(), calls=%async_computation.10 | async-start | bytes 11796480 | tf_op jit(solution)/shard_map/reduce_scatter | solution.py:136
  618.7 77.7 %collective-permute-start = (bf16[3,384,1536]{2,1,0:T(8,128)(2,1)}, bf16[3,384,1536]{2,1,0:T(8,128)(2,1)}, u32[]{:S(2)}, u32[]{:S(2)}) collective-permute-start(bf16[3,384,1536]{2,1,0:T(8,128)(2,1)} %get-tuple-element.822), channel_id=1, source_target_pairs={{0,4},{1,5},{2,6},{3,7}} | collective-permute-start | bytes 10616840 | tf_op jit(solution)/shard_map/while/body/eval_jaxpr/ppermute | solution.py:129
  626.0 80.6 %collective-permute-start.1 = (bf16[3,384,1536]{2,1,0:T(8,128)(2,1)}, bf16[3,384,1536]{2,1,0:T(8,128)(2,1)S(1)}, u32[]{:S(2)}, u32[]{:S(2)}) collective-permute-start(bf16[3,384,1536]{2,1,0:T(8,128)(2,1)} %get-tuple-element.738), channel_id=1, source_target_pairs={{4,0},{5,1},{6,2},{7,3}} | collective-permute-start | bytes 10616840 | tf_op jit(solution)/shard_map/while/body/eval_jaxpr/ppermute | solution.py:130
  891.2 78.0 %collective-permute-start = (bf16[3,384,1536]{2,1,0:T(8,128)(2,1)}, bf16[3,384,1536]{2,1,0:T(8,128)(2,1)}, u32[]{:S(2)}, u32[]{:S(2)}) collective-permute-start(bf16[3,384,1536]{2,1,0:T(8,128)(2,1)} %get-tuple-element.822), channel_id=1, source_target_pairs={{0,4},{1,5},{2,6},{3,7}} | collective-permute-start | bytes 10616840 | tf_op jit(solution)/shard_map/while/body/eval_jaxpr/ppermute | solution.py:129
  903.5 534.9 %collective-permute-start.1 = (bf16[3,384,1536]{2,1,0:T(8,128)(2,1)}, bf16[3,384,1536]{2,1,0:T(8,128)(2,1)S(1)}, u32[]{:S(2)}, u32[]{:S(2)}) collective-permute-start(bf16[3,384,1536]{2,1,0:T(8,128)(2,1)} %get-tuple-element.738), channel_id=1, source_target_pairs={{4,0},{5,1},{6,2},{7,3}} | collective-permute-start | bytes 10616840 | tf_op jit(solution)/shard_map/while/body/eval_jaxpr/ppermute | solution.py:130
  1623.0 481.4 %collective-permute-start = (bf16[3,384,1536]{2,1,0:T(8,128)(2,1)}, bf16[3,384,1536]{2,1,0:T(8,128)(2,1)}, u32[]{:S(2)}, u32[]{:S(2)}) collective-permute-start(bf16[3,384,1536]{2,1,0:T(8,128)(2,1)} %get-tuple-element.822), channel_id=1, source_target_pairs={{0,4},{1,5},{2,6},{3,7}} | collective-permute-start | bytes 10616840 | tf_op jit(solution)/shard_map/while/body/eval_jaxpr/ppermute | solution.py:129
  1630.8 49.2 copy-start.9
  1751.0 105.2 %copy-start = (bf16[3,384,1536]{2,1,0:T(8,128)(2,1)}, bf16[3,384,1536]{2,1,0:T(8,128)(2,1)S(1)}, u32[]{:S(2)}) copy-start(bf16[3,384,1536]{2,1,0:T(8,128)(2,1)S(1)} %get-tuple-element.613) | copy-start | bytes 10616836 | tf_op jit(solution)/shard_map/while/body/eval_jaxpr/cond
  1751.6 104.6 %copy-start.5 = (f32[3,384]{1,0:T(4,128)}, f32[3,384]{1,0:T(4,128)S(1)}, u32[]{:S(2)}) copy-start(f32[3,384]{1,0:T(4,128)S(1)} %fusion.165) | copy-start | bytes 13828 | tf_op jit(solution)/shard_map/while/body/eval_jaxpr/cond
  1825.1 31.1 copy-start.16
  1958.5 24.0 copy-start.3
  1958.6 24.0 copy-start.14
  1987.6 30.1 copy-start.1
  1987.6 30.1 copy-start.6
  2096.1 78.9 %collective-permute-start.1 = (bf16[3,384,1536]{2,1,0:T(8,128)(2,1)}, bf16[3,384,1536]{2,1,0:T(8,128)(2,1)S(1)}, u32[]{:S(2)}, u32[]{:S(2)}) collective-permute-start(bf16[3,384,1536]{2,1,0:T(8,128)(2,1)} %get-tuple-element.738), channel_id=1, source_target_pairs={{4,0},{5,1},{6,2},{7,3}} | collective-permute-start | bytes 10616840 | tf_op jit(solution)/shard_map/while/body/eval_jaxpr/ppermute | solution.py:130
  2359.6 481.4 %collective-permute-start = (bf16[3,384,1536]{2,1,0:T(8,128)(2,1)}, bf16[3,384,1536]{2,1,0:T(8,128)(2,1)}, u32[]{:S(2)}, u32[]{:S(2)}) collective-permute-start(bf16[3,384,1536]{2,1,0:T(8,128)(2,1)} %get-tuple-element.822), channel_id=1, source_target_pairs={{0,4},{1,5},{2,6},{3,7}} | collective-permute-start | bytes 10616840 | tf_op jit(solution)/shard_map/while/body/eval_jaxpr/ppermute | solution.py:129
  2367.5 49.2 copy-start.9
  2487.5 105.2 %copy-start = (bf16[3,384,1536]{2,1,0:T(8,128)(2,1)}, bf16[3,384,1536]{2,1,0:T(8,128)(2,1)S(1)}, u32[]{:S(2)}) copy-start(bf16[3,384,1536]{2,1,0:T(8,128)(2,1)S(1)} %get-tuple-element.613) | copy-start | bytes 10616836 | tf_op jit(solution)/shard_map/while/body/eval_jaxpr/cond
  2488.1 104.6 %copy-start.5 = (f32[3,384]{1,0:T(4,128)}, f32[3,384]{1,0:T(4,128)S(1)}, u32[]{:S(2)}) copy-start(f32[3,384]{1,0:T(4,128)S(1)} %fusion.165) | copy-start | bytes 13828 | tf_op jit(solution)/shard_map/while/body/eval_jaxpr/cond
  2561.6 31.1 copy-start.16
  2695.1 24.0 copy-start.3
  2724.1 30.1 copy-start.1
  2724.1 30.1 copy-start.6
  2832.6 77.8 %collective-permute-start.1 = (bf16[3,384,1536]{2,1,0:T(8,128)(2,1)}, bf16[3,384,1536]{2,1,0:T(8,128)(2,1)S(1)}, u32[]{:S(2)}, u32[]{:S(2)}) collective-permute-start(bf16[3,384,1536]{2,1,0:T(8,128)(2,1)} %get-tuple-element.738), channel_id=1, source_target_pairs={{4,0},{5,1},{6,2},{7,3}} | collective-permute-start | bytes 10616840 | tf_op jit(solution)/shard_map/while/body/eval_jaxpr/ppermute | solution.py:130
  2931.1 642.9 %collective-permute-start = (bf16[3,384,1536]{2,1,0:T(8,128)(2,1)}, bf16[3,384,1536]{2,1,0:T(8,128)(2,1)}, u32[]{:S(2)}, u32[]{:S(2)}) collective-permute-start(bf16[3,384,1536]{2,1,0:T(8,128)(2,1)} %get-tuple-element.822), channel_id=1, source_target_pairs={{0,4},{1,5},{2,6},{3,7}} | collective-permute-start | bytes 10616840 | tf_op jit(solution)/shard_map/while/body/eval_jaxpr/ppermute | solution.py:129
  3102.8 49.2 copy-start.9
  3222.7 105.4 %copy-start = (bf16[3,384,1536]{2,1,0:T(8,128)(2,1)}, bf16[3,384,1536]{2,1,0:T(8,128)(2,1)S(1)}, u32[]{:S(2)}) copy-start(bf16[3,384,1536]{2,1,0:T(8,128)(2,1)S(1)} %get-tuple-element.613) | copy-start | bytes 10616836 | tf_op jit(solution)/shard_map/while/body/eval_jaxpr/cond
  3223.3 104.9 %copy-start.5 = (f32[3,384]{1,0:T(4,128)}, f32[3,384]{1,0:T(4,128)S(1)}, u32[]{:S(2)}) copy-start(f32[3,384]{1,0:T(4,128)S(1)} %fusion.165) | copy-start | bytes 13828 | tf_op jit(solution)/shard_map/while/body/eval_jaxpr/cond
  3296.8 31.3 copy-start.16
  3459.5 30.1 copy-start.1
  3459.5 30.1 copy-start.6
  3567.7 76.6 %collective-permute-start.1 = (bf16[3,384,1536]{2,1,0:T(8,128)(2,1)}, bf16[3,384,1536]{2,1,0:T(8,128)(2,1)S(1)}, u32[]{:S(2)}, u32[]{:S(2)}) collective-permute-start(bf16[3,384,1536]{2,1,0:T(8,128)(2,1)} %get-tuple-element.738), channel_id=1, source_target_pairs={{4,0},{5,1},{6,2},{7,3}} | collective-permute-start | bytes 10616840 | tf_op jit(solution)/shard_map/while/body/eval_jaxpr/ppermute | solution.py:130
  3665.1 479.3 %collective-permute-start = (bf16[3,384,1536]{2,1,0:T(8,128)(2,1)}, bf16[3,384,1536]{2,1,0:T(8,128)(2,1)}, u32[]{:S(2)}, u32[]{:S(2)}) collective-permute-start(bf16[3,384,1536]{2,1,0:T(8,128)(2,1)} %get-tuple-element.822), channel_id=1, source_target_pairs={{0,4},{1,5},{2,6},{3,7}} | collective-permute-start | bytes 10616840 | tf_op jit(solution)/shard_map/while/body/eval_jaxpr/ppermute | solution.py:129
  3672.9 49.2 copy-start.9
  3793.0 105.2 %copy-start = (bf16[3,384,1536]{2,1,0:T(8,128)(2,1)}, bf16[3,384,1536]{2,1,0:T(8,128)(2,1)S(1)}, u32[]{:S(2)}) copy-start(bf16[3,384,1536]{2,1,0:T(8,128)(2,1)S(1)} %get-tuple-element.613) | copy-start | bytes 10616836 | tf_op jit(solution)/shard_map/while/body/eval_jaxpr/cond
  3793.6 104.6 %copy-start.5 = (f32[3,384]{1,0:T(4,128)}, f32[3,384]{1,0:T(4,128)S(1)}, u32[]{:S(2)}) copy-start(f32[3,384]{1,0:T(4,128)S(1)} %fusion.165) | copy-start | bytes 13828 | tf_op jit(solution)/shard_map/while/body/eval_jaxpr/cond
  3867.1 31.1 copy-start.16
  4029.6 30.1 copy-start.1
  4029.6 30.1 copy-start.6
  4138.1 75.5 %collective-permute-start.1 = (bf16[3,384,1536]{2,1,0:T(8,128)(2,1)}, bf16[3,384,1536]{2,1,0:T(8,128)(2,1)S(1)}, u32[]{:S(2)}, u32[]{:S(2)}) collective-permute-start(bf16[3,384,1536]{2,1,0:T(8,128)(2,1)} %get-tuple-element.738), channel_id=1, source_target_pairs={{4,0},{5,1},{6,2},{7,3}} | collective-permute-start | bytes 10616840 | tf_op jit(solution)/shard_map/while/body/eval_jaxpr/ppermute | solution.py:130
  4216.7 231.9 %reduce-scatter.14.cloned.1.call-start = ((), (), s32[]{:S(2)}) async-start(), calls=%async_computation.13 | async-start | bytes 21233664 | tf_op jit(solution)/shard_map/reduce_scatter | solution.py:138
  4222.6 417.1 %reduce-scatter.6.cloned.1.call-start = ((), (), s32[]{:S(2)}) async-start(), calls=%async_computation.9 | async-start | bytes 35389440 | tf_op jit(solution)/shard_map/reduce_scatter | solution.py:136
  4223.4 670.8 %reduce-scatter.10.cloned.1.call-start = ((), (), s32[]{:S(2)}) async-start(), calls=%async_computation.11 | async-start | bytes 47185920 | tf_op jit(solution)/shard_map/reduce_scatter | solution.py:136
  4224.1 924.4 %reduce-scatter.12.cloned.1.call-start = ((), (), s32[]{:S(2)}) async-start(), calls=%async_computation.12 | async-start | bytes 47185920 | tf_op jit(solution)/shard_map/reduce_scatter | solution.py:136
  (55 other events, 499.4 us)
Sparse Core Ops, SparseCore 0:
  9.5 37.3 all-gather.6
  48.4 88.8 all-gather.4
  138.8 118.0 all-gather.8
  258.3 118.0 all-gather.10
  4216.8 70.3 reduce-scatter.7
  4290.0 158.6 reduce-scatter.13
  4451.8 187.9 reduce-scatter.5
  4642.8 251.2 reduce-scatter.9
  4897.2 251.2 reduce-scatter.11
where the time goes:
time: 5160 us
  waiting for transfers between devices  2170 us (42%)
  matrix products  2060 us (40%)
  other arithmetic  539 us (10%)
  starting transfers between devices  197 us (4%)
  local copies, waits for them, and re-layouts  139 us (3%)
    reduce_scatter x4, waiting for transfers between devices, device_step(): lax.psum_scatter(acc_part, 'dp', scatter_dimension=1, tiled=True)  762 us
    ppermute x6, waiting for transfers between devices, run_tick(): bwd_buf = lax.ppermute(ct_in, 'pp', bwd_pairs)  759 us
    all_gather x4, waiting for transfers between devices, device_step(): lax.all_gather(w_part, 'dp', axis=1, tiled=True)  366 us
    sub x12, other arithmetic, attn_core(): jax.nn.softmax(jnp.where(causal, scores, -1e+30), axis=-1)  325 us
    dot_general x16, matrix products, attn_core(): jnp.einsum('bqnh,bknh->bnqk', q_heads, k_heads, preferred_element_type=jn...  286 us
    dot_general x8, matrix products, layer_forward(): jnp.einsum('bsd,df->bsf', normed2, w_up, preferred_element_type=jnp.float32)  245 us
    dot_general x16, matrix products, attn_core(): jnp.einsum('bnqk,bknh->bqnh', prob_bf, v_heads, preferred_element_type=jn...  218 us
    dot_general x8, matrix products, layer_forward(): jnp.einsum('bsd,dnh->bsnh', normed, w_qkv, preferred_element_type=jnp.flo...  201 us
  transfers between devices with their start and end apart: 21, of which 17 were waited for; matrix products, arithmetic and copies ran while one was open for 37% of the time, Pallas kernels for 0%

commit v1 on v0

v1 whole, which is shorter than its diff:
```python
import functools

import jax
import jax.numpy as jnp
from jax import lax
from jax.experimental import pallas as pl
from jax.experimental.pallas import tpu as pltpu
from jax.sharding import PartitionSpec as P


NORM_EPS = 1e-6
BF16, F32 = jnp.bfloat16, jnp.float32
HEAD = 96
GROUP = 4 * HEAD
LOG2E = 1.4426950408889634
WINDOWS = ((0, 128), (0, 256), (128, 384), (256, 384))


def dot_nn(lhs, rhs):
    return lax.dot_general(lhs, rhs, (((1,), (0,)), ((), ())), preferred_element_type=F32)


def dot_nt(lhs, rhs):
    return lax.dot_general(lhs, rhs, (((1,), (1,)), ((), ())), preferred_element_type=F32)


def dot_tn(lhs, rhs):
    return lax.dot_general(lhs, rhs, (((0,), (0,)), ((), ())), preferred_element_type=F32)


def head_mask(rows, head):
    first, last = WINDOWS[head]
    lane = lax.broadcasted_iota(jnp.int32, (rows, last - first), 1) + first
    return (lane >= head * HEAD) & (lane < (head + 1) * HEAD)


def only(mask, value):
    return jnp.where(mask, value, jnp.zeros_like(value))


def join_windows(parts):
    return jnp.concatenate([
        parts[0] + parts[1][:, :128],
        parts[1][:, 128:] + parts[2][:, :128],
        parts[2][:, 128:] + parts[3],
    ], axis=1)


def attn_fwd_kernel(seq, width, qkv_ref, out_ref):
    scale = HEAD ** -0.5
    block = 128

    def one_group(group, carry):
        first = pl.multiple_of(group * GROUP, 128)
        heads_out = []
        for head in range(4):
            lo, hi = WINDOWS[head]
            q_win = qkv_ref[:, pl.ds(first + lo, hi - lo)]
            mask = head_mask(seq, head)
            k_win = only(mask, qkv_ref[:, pl.ds(width + first + lo, hi - lo)])
            v_win = only(mask, qkv_ref[:, pl.ds(2 * width + first + lo, hi - lo)])
            rows_out = []
            for start in range(0, seq, block):
                keys = start + block
                scores = dot_nt(q_win[start:keys], k_win[:keys])
                row = lax.broadcasted_iota(jnp.int32, (block, keys), 0) + start
                col = lax.broadcasted_iota(jnp.int32, (block, keys), 1)
                scores = jnp.where(row >= col, scores, -1e30)
                top = jnp.max(scores, axis=1, keepdims=True)
                weight = jnp.exp2((scores - top) * (scale * LOG2E))
                prob = weight * (1.0 / jnp.sum(weight, axis=1, keepdims=True))
                rows_out.append(dot_nn(prob.astype(BF16), v_win[:keys]))
            heads_out.append(jnp.concatenate(rows_out, axis=0))
        out_ref[:, pl.ds(first, GROUP)] = join_windows(heads_out).astype(BF16)
        return carry

    lax.fori_loop(0, width // GROUP, one_group, 0)


def attn_bwd_kernel(seq, width, qkv_ref, ct_ref, out_ref):
    scale = HEAD ** -0.5
    blocks = ((0, 256), (256, seq))

    def one_group(group, carry):
        first = pl.multiple_of(group * GROUP, 128)
        ct_q, ct_k, ct_v = [], [], []
        for head in range(4):
            lo, hi = WINDOWS[head]
            mask = head_mask(seq, head)
            q_win = qkv_ref[:, pl.ds(first + lo, hi - lo)]
            ct_win = ct_ref[:, pl.ds(first + lo, hi - lo)]
            q_own, ct_own = only(mask, q_win), only(mask, ct_win)
            k_own = only(mask, qkv_ref[:, pl.ds(width + first + lo, hi - lo)])
            v_own = only(mask, qkv_ref[:, pl.ds(2 * width + first + lo, hi - lo)])
            head_q, head_k, head_v = [], None, None
            for start, stop in blocks:
                keys = stop
                scores = dot_nt(k_own[:keys], q_win[start:stop])
                key = lax.broadcasted_iota(jnp.int32, (keys, stop - start), 0)
                query = lax.broadcasted_iota(jnp.int32, (keys, stop - start), 1) + start
                scores = jnp.where(query >= key, scores, -1e30)
                top = jnp.max(scores, axis=0, keepdims=True)
                weight = jnp.exp2((scores - top) * (scale * LOG2E))
                prob = weight * (1.0 / jnp.sum(weight, axis=0, keepdims=True))
                ct_prob = dot_nt(v_own[:keys], ct_win[start:stop]).astype(BF16).astype(F32)
                inner = prob * ct_prob
                ct_score = ((inner - prob * jnp.sum(inner, axis=0, keepdims=True)) * scale).astype(BF16)
                part_v = dot_nn(prob.astype(BF16), ct_own[start:stop])
                part_k = dot_nn(ct_score, q_own[start:stop])
                head_q.append(dot_tn(ct_score, k_own[:keys]))
                if head_k is None:
                    head_k, head_v = part_k, part_v
                else:
                    old = head_k.shape[0]
                    head_k = jnp.concatenate([head_k + part_k[:old], part_k[old:]], axis=0)
                    head_v = jnp.concatenate([head_v + part_v[:old], part_v[old:]], axis=0)
            ct_q.append(jnp.concatenate(head_q, axis=0))
            ct_k.append(head_k)
            ct_v.append(head_v)
        out_ref[:, pl.ds(first, GROUP)] = join_windows(ct_q).astype(BF16)
        out_ref[:, pl.ds(width + first, GROUP)] = join_windows(ct_k).astype(BF16)
        out_ref[:, pl.ds(2 * width + first, GROUP)] = join_windows(ct_v).astype(BF16)
        return carry

    lax.fori_loop(0, width // GROUP, one_group, 0)


def attention(qkv, seq):
    rows, width = qkv.shape[0], qkv.shape[1] // 3
    flops = 4 * rows * seq * width
    return pl.pallas_call(
        functools.partial(attn_fwd_kernel, seq, width),
        grid=(rows // seq,),
        in_specs=[pl.BlockSpec((seq, 3 * width), lambda i: (i, 0))],
        out_specs=pl.BlockSpec((seq, width), lambda i: (i, 0)),
        out_shape=jax.ShapeDtypeStruct((rows, width), BF16),
        cost_estimate=pl.CostEstimate(flops=flops, bytes_accessed=8 * rows * width, transcendentals=rows * seq * 16),
        compiler_params=pltpu.CompilerParams(vmem_limit_bytes=40 << 20),
        name='attn_fwd',
    )(qkv)


def attention_pull(qkv, ct_heads, seq):
    rows, width = qkv.shape[0], qkv.shape[1] // 3
    flops = 10 * rows * seq * width
    return pl.pallas_call(
        functools.partial(attn_bwd_kernel, seq, width),
        grid=(rows // seq,),
        in_specs=[pl.BlockSpec((seq, 3 * width), lambda i: (i, 0)), pl.BlockSpec((seq, width), lambda i: (i, 0))],
        out_specs=pl.BlockSpec((seq, 3 * width), lambda i: (i, 0)),
        out_shape=jax.ShapeDtypeStruct((rows, 3 * width), BF16),
        cost_estimate=pl.CostEstimate(flops=flops, bytes_accessed=14 * rows * width, transcendentals=rows * seq * 16),
        compiler_params=pltpu.CompilerParams(vmem_limit_bytes=48 << 20),
        name='attn_bwd',
    )(qkv, ct_heads)


def rms_norm(hidden):
    return hidden * lax.rsqrt(jnp.mean(hidden * hidden, axis=-1, keepdims=True) + NORM_EPS)


def rms_pull(hidden, ct_normed):
    return jax.vjp(rms_norm, hidden.astype(F32))[1](ct_normed.astype(F32))[0]


def gelu_tanh(pre_act):
    return jax.nn.gelu(pre_act, approximate=True)


def block_forward(hidden, weights, seq):
    w_qkv, w_proj, w_up, _ = weights
    hid_f32 = hidden.astype(F32)
    normed = rms_norm(hid_f32).astype(BF16)
    qkv = dot_nn(normed, w_qkv).astype(BF16)
    heads = attention(qkv, seq)
    mid = (hid_f32 + dot_nn(heads, w_proj)).astype(BF16)
    normed2 = rms_norm(mid.astype(F32)).astype(BF16)
    up_act = dot_nn(normed2, w_up).astype(BF16)
    gelu_out = gelu_tanh(up_act.astype(F32)).astype(BF16)
    return hidden, normed, qkv, heads, mid, normed2, up_act, gelu_out


def block_output(saved, w_down):
    return (saved[4].astype(F32) + dot_nn(saved[7], w_down)).astype(BF16)


def block_backward(saved, ct_out, weights, seq, tag):
    w_qkv, w_proj, w_up, w_down = weights
    hidden, normed, qkv, heads, mid, normed2, up_act, gelu_out = saved
    g_down, ct_out = lax.optimization_barrier((dot_tn(gelu_out, ct_out), ct_out))
    ct_gelu = dot_nt(ct_out, w_down).astype(BF16)
    ct_up = jax.vjp(gelu_tanh, up_act.astype(F32))[1](ct_gelu.astype(F32))[0].astype(BF16)
    g_up, ct_up = lax.optimization_barrier((dot_tn(normed2, ct_up), ct_up))
    ct_norm2 = dot_nt(ct_up, w_up).astype(BF16)
    ct_mid = (ct_out.astype(F32) + rms_pull(mid, ct_norm2)).astype(BF16)
    g_proj, ct_mid = lax.optimization_barrier((dot_tn(heads, ct_mid), ct_mid))
    ct_heads = dot_nt(ct_mid, w_proj).astype(BF16)
    ct_qkv = attention_pull(qkv, ct_heads, seq)
    g_qkv, ct_qkv = lax.optimization_barrier((dot_tn(normed, ct_qkv), ct_qkv))
    ct_hidden = None
    if tag:
        ct_norm = dot_nt(ct_qkv, w_qkv).astype(BF16)
        ct_hidden = (ct_mid.astype(F32) + rms_pull(hidden, ct_norm)).astype(BF16)
    return ct_hidden, (g_qkv, g_proj, g_up, g_down)


def solution(mesh):
    swap = [(0, 1), (1, 0)]
    both = ('dp', 'pp')

    def whole_step(act_in, loss_seed, w_qkv, w_proj, w_up, w_down):
        row = lax.axis_index('pp')
        num_micro, batch, seq, width = act_in.shape
        half_micro = num_micro // 2

        def mine(array):
            return lax.dynamic_slice_in_dim(array, row * half_micro, half_micro, 0).reshape(-1, width)

        def halves(shard):
            half = shard.shape[0] // 2
            kept = lax.dynamic_slice_in_dim(shard, row * half, half, 0)
            sent = lax.dynamic_slice_in_dim(shard, (1 - row) * half, half, 0)
            got = lax.ppermute(sent, 'pp', swap)
            return jnp.where(row == 0, kept, got), jnp.where(row == 0, got, kept)

        def gather(part):
            return lax.all_gather(part, both, axis=0, tiled=True)

        shard_qkv = w_qkv[0].reshape(w_qkv.shape[1], -1)
        qkv_both = lax.all_gather(shard_qkv, ('pp', 'dp'), axis=0, tiled=True)
        parts = [halves(shard[0]) for shard in (w_proj, w_up, w_down)]
        weights = []
        for idx in range(2):
            weights.append((qkv_both[idx * width:(idx + 1) * width],) + tuple(gather(part[idx]) for part in parts))

        hidden, seed = mine(act_in), mine(loss_seed)
        saved0 = block_forward(hidden, weights[0], seq)
        hidden1 = block_output(saved0, weights[0][3])
        saved1 = block_forward(hidden1, weights[1], seq)
        ct_mid, grads1 = block_backward(saved1, seed, weights[1], seq, 1)
        _, grads0 = block_backward(saved0, ct_mid, weights[0], seq, 0)
        out = block_output(saved1, weights[1][3]).reshape(half_micro, batch, seq, width)

        def reduce(grad):
            return lax.psum_scatter(grad, both, scatter_dimension=0, tiled=True)

        sums1 = [reduce(grads1[i]) for i in (3, 2, 1, 0)]
        sums0 = [reduce(grads0[i]) for i in (3, 2, 1, 0)]

        def settle(sum0, sum1):
            kept = jnp.where(row == 0, sum0, sum1)
            got = lax.ppermute(jnp.where(row == 0, sum1, sum0), 'pp', swap)
            return lax.dynamic_update_slice_in_dim(jnp.concatenate([kept, kept]), got, (1 - row) * got.shape[0], 0)

        g_down, g_up, g_proj, g_qkv = [settle(sum0, sum1)[None] for sum0, sum1 in zip(sums0, sums1)]

        half = seq // 2
        kept = lax.dynamic_slice_in_dim(out, row * half, half, 2)
        got = lax.ppermute(lax.dynamic_slice_in_dim(out, (1 - row) * half, half, 2), 'pp', swap)
        act_out = lax.dynamic_update_slice_in_dim(jnp.concatenate([kept, kept]), got, (1 - row) * half_micro, 0)
        return g_qkv.reshape(w_qkv.shape), g_proj, g_up, g_down, act_out

    weight_spec = P('pp', 'dp')
    act_spec = P(None, 'dp')
    return jax.shard_map(whole_step, mesh=mesh, in_specs=(act_spec, act_spec, weight_spec, weight_spec, weight_spec, weight_spec), out_specs=(weight_spec, weight_spec, weight_spec, weight_spec, P(None, 'dp', 'pp')), check_vma=False)
```

time: 5160 us -> 3070 us (0.59)
  matrix products: 2060 us -> 1060 us
  waiting for transfers between devices: 2170 us -> 1480 us
  other arithmetic: 539 us -> 98.2 us
  Pallas kernels: 0 us -> 333 us
  starting transfers between devices: 197 us -> 14.2 us
  local copies, waits for them, and re-layouts: 139 us -> 65.2 us
    dot_general x92 -> x23, matrix products: 2060 us -> 1060 us  [the longest x7 372 us: dot_nt(): lax.dot_general(lhs, rhs, (((1,), (1,)), ((), ())), preferred_element_typ...]
    ppermute x12 -> x8, waiting for transfers between devices: 878 us -> 386 us  [the longest x3 211 us: halves(): got = lax.ppermute(sent, 'pp', swap)]
    all_gather x4 -> x7, waiting for transfers between devices: 366 us -> 0.07 us  [the longest x6 0.05 us: gather(): return lax.all_gather(part, both, axis=0, tiled=True)]
    pallas_call x0 -> x4, Pallas kernels: none -> 333 us  [the longest x2 181 us: attention(): pl.pallas_call(functools.partial(attn_fwd_kernel, seq, width), grid=(rows...]
    sub x12 -> x0, other arithmetic: 325 us -> none  [attn_core(): jax.nn.softmax(jnp.where(causal, scores, -1e+30), axis=-1)]
    ppermute x12 -> x8, starting transfers between devices: 196 us -> 13.4 us  [the longest x3 8.32 us: halves(): got = lax.ppermute(sent, 'pp', swap)]
    reduce_scatter x5 -> x8, waiting for transfers between devices: 924 us -> 1090 us  [reduce(): return lax.psum_scatter(grad, both, scatter_dimension=0, tiled=True)]
    convert_element_type x12 -> x4, other arithmetic: 103 us -> 33.1 us  [the longest x2 18.3 us: block_backward(): ct_mid = (ct_out.astype(F32) + rms_pull(mid, ct_norm2)).astype(BF16)]
  transfers between devices with their start and end apart: 21 -> 23, of which waited for: 17 -> 10; matrix products, arithmetic and copies ran while one was open for 37% -> 32% of each run, Pallas kernels for 0% -> 11%
where the time goes in v1:
time: 3070 us; the launch traced here: 3060 us
  waiting for transfers between devices  1480 us (48%)
  matrix products  1060 us (35%)
  Pallas kernels  333 us (11%)
  other arithmetic  98.2 us (3%)
  local copies, waits for them, and re-layouts  65.2 us (2%)
    reduce_scatter x8, waiting for transfers between devices, reduce(): return lax.psum_scatter(grad, both, scatter_dimension=0, tiled=True)  1090 us
    dot_general x7, matrix products, dot_nt(): lax.dot_general(lhs, rhs, (((1,), (1,)), ((), ())), preferred_element_typ...  372 us
    dot_general x8, matrix products, dot_tn(): lax.dot_general(lhs, rhs, (((0,), (0,)), ((), ())), preferred_element_typ...  343 us
    dot_general x8, matrix products, dot_nn(): lax.dot_general(lhs, rhs, (((1,), (0,)), ((), ())), preferred_element_typ...  341 us
    ppermute x3, waiting for transfers between devices, halves(): got = lax.ppermute(sent, 'pp', swap)  211 us
    pallas_call x2, Pallas kernels, attention(): pl.pallas_call(functools.partial(attn_fwd_kernel, seq, width), grid=(rows...  181 us
    pallas_call x2, Pallas kernels, attention_pull(): pl.pallas_call(functools.partial(attn_bwd_kernel, seq, width), grid=(rows...  151 us
    ppermute x1, waiting for transfers between devices, whole_step(): lax.ppermute(lax.dynamic_slice_in_dim(out, (1 - row) * half, half, 2), 'p...  109 us
  transfers between devices with their start and end apart: 23, of which 10 were waited for; matrix products, arithmetic and copies ran while one was open for 32% of the time, Pallas kernels for 11%

profile of v1, /device:TPU:0, one launch (start us, length us, event | category | flops | bytes accessed | tf_op | source)
XLA Modules:
  0.0 3060.2 jit_solution(7363240247318128789)
XLA Ops:
  12.4 17.2 collective-permute-done
  36.3 96.1 %collective-permute-done.1 = bf16[192,6144]{1,0:T(8,128)(2,1)S(1)} collective-permute-done((bf16[192,6144]{1,0:T(8,128)(2,1)S(1)}, bf16[192,6144]{1,0:T(8,128)(2,1)S(1)}, u32[]{:S(2)}, u32[]{:S(2)}) %collective-permute-start.1) | collective-permute-done | bytes 2359328 | tf_op jit(solution)/shard_map/ppermute | solution.py:223
  143.1 97.5 %collective-permute-done.2 = bf16[768,1536]{1,0:T(8,128)(2,1)S(1)} collective-permute-done((bf16[768,1536]{1,0:T(8,128)(2,1)}, bf16[768,1536]{1,0:T(8,128)(2,1)S(1)}, u32[]{:S(2)}, u32[]{:S(2)}) %collective-permute-start.2) | collective-permute-done | bytes 2359328 | tf_op jit(solution)/shard_map/ppermute | solution.py:223
  251.5 6.8 constant_dynamic-slice_fusion.3
  258.3 6.8 constant_dynamic-slice_fusion.2
  265.1 7.4 fusion.40
  272.7 40.0 %convolution_convert_fusion.5.qkv_ref = bf16[2304,4608]{1,0:T(8,128)(2,1)} fusion(bf16[2304,1536]{1,0:T(8,128)(2,1)} %fusion.40, bf16[3072,4608]{0,1:T(8,128)(2,1)} %all-gather.8.cloned.1.call-done), kind=kOutput, calls=%fused_computation.39 | convolution fusion | flops 32625524736 | bytes 42467328 | tf_op jit(solution)/shard_map/dot_general | solution.py:20
  312.7 90.7 %attn_fwd.2 = bf16[2304,1536]{1,0:T(8,128)(2,1)S(1)} custom-call(bf16[2304,4608]{1,0:T(8,128)(2,1)} %convolution_convert_fusion.5.qkv_ref), custom_call_target="tpu_custom_call" | custom-call | flops 5435817984 | bytes 28311552 | tf_op jit(solution)/shard_map/attn_fwd/pallas_call | solution.py:131
  406.4 18.1 fusion.28
  425.2 52.3 %convolution_convert_fusion.3 = bf16[2304,6144]{1,0:T(8,128)(2,1)} fusion(bf16[1536,6144]{1,0:T(8,128)(2,1)} %all-gather.12.cloned.1.call-done, bf16[2304,1536]{1,0:T(8,128)(2,1)} %get-tuple-element.57, f32[2304]{0:T(1024)S(1)} %fusion.59), kind=kOutput, calls=%fused_computation.37 | convolution fusion | flops 43511316480 | bytes 54273024 | tf_op jit(solution)/shard_map/dot_general | solution.py:20
  477.5 59.5 %fusion.31 = (f32[2304]{0:T(1024)S(1)}, bf16[2304,1536]{1,0:T(8,128)(2,1)S(1)}) fusion(bf16[6144,1536]{1,0:T(8,128)(2,1)} %all-gather.14.cloned.1.call-done, bf16[2304,6144]{1,0:T(8,128)(2,1)} %convolution_convert_fusion.3, bf16[2304,1536]{1,0:T(8,128)(2,1)} %get-tuple-element.57), kind=kOutput, calls=%fused_computation.70 | convolution fusion | flops 43649331200 | bytes 61350912 | tf_op jit(solution)/shard_map/dot_general | solution.py:20
  537.0 41.3 %convolution_convert_fusion.4.qkv_ref = bf16[2304,4608]{1,0:T(8,128)(2,1)} fusion(bf16[3072,4608]{0,1:T(8,128)(2,1)} %all-gather.8.cloned.1.call-done, bf16[2304,1536]{1,0:T(8,128)(2,1)S(1)} %get-tuple-element.59, f32[2304]{0:T(1024)S(1)} %fusion.60), kind=kOutput, calls=%fused_computation.38 | convolution fusion | flops 32636141568 | bytes 42476544 | tf_op jit(solution)/shard_map/dot_general | solution.py:20
  578.3 90.7 %attn_fwd.3 = bf16[2304,1536]{1,0:T(8,128)(2,1)S(1)} custom-call(bf16[2304,4608]{1,0:T(8,128)(2,1)} %convolution_convert_fusion.4.qkv_ref), custom_call_target="tpu_custom_call" | custom-call | flops 5435817984 | bytes 28311552 | tf_op jit(solution)/shard_map/attn_fwd/pallas_call | solution.py:131
  672.0 18.5 fusion.35
  691.1 52.3 %convolution_convert_fusion.2 = bf16[2304,6144]{1,0:T(8,128)(2,1)} fusion(bf16[1536,6144]{1,0:T(8,128)(2,1)} %all-gather.18.cloned.1.call-done, bf16[2304,1536]{1,0:T(8,128)(2,1)} %get-tuple-element.61, f32[2304]{0:T(1024)S(1)} %fusion.61), kind=kOutput, calls=%fused_computation.36 | convolution fusion | flops 43511316480 | bytes 54273024 | tf_op jit(solution)/shard_map/dot_general | solution.py:20
  743.4 60.1 %fusion.63 = f32[6144,1536]{1,0:T(8,128)} fusion(bf16[2304,1536]{1,0:T(8,128)(2,1)S(1)} %bitcast.82, bf16[2304,6144]{1,0:T(8,128)(2,1)} %convolution_convert_fusion.2), kind=kOutput, calls=%fused_computation.138 | convolution fusion | flops 43628101632 | bytes 73138176 | tf_op jit(solution)/shard_map/dot_general | solution.py:28
  803.5 86.7 %fusion.4 = bf16[2304,6144]{1,0:T(8,128)(2,1)} fusion(bf16[2304,6144]{1,0:T(8,128)(2,1)} %convolution_convert_fusion.2, bf16[2304,1536]{1,0:T(8,128)(2,1)} %bitcast.78, bf16[6144,1536]{1,0:T(8,128)(2,1)} %all-gather.20.cloned.1.call-done), kind=kOutput, calls=%fused_computation.16 | convolution fusion | flops 43812126720 | bytes 82575360 | tf_op jit(solution)/shard_map/dot_general | solution.py:24
  890.3 53.7 %fusion.50 = f32[1536,6144]{1,0:T(8,128)} fusion(bf16[2304,6144]{1,0:T(8,128)(2,1)} %fusion.4, bf16[2304,1536]{1,0:T(8,128)(2,1)} %get-tuple-element.61, f32[2304]{0:T(1024)S(1)} %copy-done.15), kind=kOutput, calls=%fused_computation.100 | convolution fusion | flops 43497160704 | bytes 73147392 | tf_op jit(solution)/shard_map/dot_general | solution.py:28
  944.0 61.5 %fusion.37 = (f32[2304]{0:T(1024)S(1)}, bf16[2304,1536]{1,0:T(8,128)(2,1)}) fusion(bf16[2304,1536]{1,0:T(8,128)(2,1)} %get-tuple-element.61, bf16[2304,6144]{1,0:T(8,128)(2,1)} %fusion.4, bf16[1536,6144]{1,0:T(8,128)(2,1)} %all-gather.18.cloned.1.call-done), kind=kOutput, calls=%fused_computation.76 | convolution fusion | flops 43504234496 | bytes 61350912 | tf_op jit(solution)/shard_map/dot_general | solution.py:24
  1005.5 9.1 fusion.23
  1017.5 14.6 fusion.68
  1032.2 16.6 convolution_convert_fusion.9.ct_ref
  1048.8 75.6 %attn_bwd.2 = bf16[2304,4608]{1,0:T(8,128)(2,1)} custom-call(bf16[2304,4608]{1,0:T(8,128)(2,1)} %convolution_convert_fusion.4.qkv_ref, bf16[2304,1536]{1,0:T(8,128)(2,1)} %convolution_convert_fusion.9.ct_ref), custom_call_target="tpu_custom_call" | custom-call | flops 13589544960 | bytes 49545216 | tf_op jit(solution)/shard_map/attn_bwd/pallas_call | solution.py:146
  1124.4 42.5 %fusion.53 = f32[1536,4608]{1,0:T(8,128)} fusion(bf16[2304,4608]{1,0:T(8,128)(2,1)} %attn_bwd.2, bf16[2304,1536]{1,0:T(8,128)(2,1)} %copy-done.6, f32[2304]{0:T(1024)S(1)} %copy-done.13), kind=kOutput, calls=%fused_computation.101 | convolution fusion | flops 32625524736 | bytes 56632320 | tf_op jit(solution)/shard_map/dot_general | solution.py:28
  1166.9 41.8 %fusion.34 = (f32[2304]{0:T(1024)S(1)}, bf16[2304,1536]{1,0:T(8,128)(2,1)}) fusion(bf16[2304,1536]{1,0:T(8,128)(2,1)} %copy-done.6, bf16[2304,4608]{1,0:T(8,128)(2,1)} %attn_bwd.2, bf16[3072,4608]{0,1:T(8,128)(2,1)} %all-gather.8.cloned.1.call-done), kind=kOutput, calls=%fused_computation.73 | convolution fusion | flops 32632600576 | bytes 49554432 | tf_op jit(solution)/shard_map/dot_general | solution.py:24
  1208.8 7.4 fusion.25
  1219.0 60.2 %fusion.65 = f32[6144,1536]{1,0:T(8,128)} fusion(bf16[2304,1536]{1,0:T(8,128)(2,1)S(1)} %fusion.25, bf16[2304,6144]{1,0:T(8,128)(2,1)} %convolution_convert_fusion.3), kind=kOutput, calls=%fused_computation.139 | convolution fusion | flops 43628101632 | bytes 73138176 | tf_op jit(solution)/shard_map/dot_general | solution.py:28
  1279.2 86.7 %fusion.7 = bf16[2304,6144]{1,0:T(8,128)(2,1)} fusion(bf16[2304,6144]{1,0:T(8,128)(2,1)} %convolution_convert_fusion.3, bf16[2304,1536]{1,0:T(8,128)(2,1)} %copy-done.5, bf16[6144,1536]{1,0:T(8,128)(2,1)} %all-gather.14.cloned.1.call-done), kind=kOutput, calls=%fused_computation.19 | convolution fusion | flops 43812126720 | bytes 82575360 | tf_op jit(solution)/shard_map/dot_general | solution.py:24
  1366.0 53.8 %fusion.56 = f32[1536,6144]{1,0:T(8,128)} fusion(bf16[2304,6144]{1,0:T(8,128)(2,1)} %fusion.7, bf16[2304,1536]{1,0:T(8,128)(2,1)} %get-tuple-element.57, f32[2304]{0:T(1024)S(1)} %copy-done.11), kind=kOutput, calls=%fused_computation.102 | convolution fusion | flops 43497160704 | bytes 73147392 | tf_op jit(solution)/shard_map/dot_general | solution.py:28
  1419.8 61.5 %fusion.30 = (f32[2304]{0:T(1024)S(1)}, bf16[2304,1536]{1,0:T(8,128)(2,1)}) fusion(bf16[2304,1536]{1,0:T(8,128)(2,1)} %get-tuple-element.57, bf16[2304,6144]{1,0:T(8,128)(2,1)} %fusion.7, bf16[1536,6144]{1,0:T(8,128)(2,1)} %all-gather.12.cloned.1.call-done), kind=kOutput, calls=%fused_computation.69 | convolution fusion | flops 43504234496 | bytes 61350912 | tf_op jit(solution)/shard_map/dot_general | solution.py:24
  1481.4 9.1 fusion.27
  1493.4 14.6 fusion.69
  1508.6 17.5 convolution_convert_fusion.8.ct_ref
  1526.1 75.9 %attn_bwd.3 = bf16[2304,4608]{1,0:T(8,128)(2,1)} custom-call(bf16[2304,4608]{1,0:T(8,128)(2,1)} %convolution_convert_fusion.5.qkv_ref, bf16[2304,1536]{1,0:T(8,128)(2,1)} %convolution_convert_fusion.8.ct_ref), custom_call_target="tpu_custom_call" | custom-call | flops 13589544960 | bytes 49545216 | tf_op jit(solution)/shard_map/attn_bwd/pallas_call | solution.py:146
  1602.0 43.9 %fusion.70 = f32[1536,4608]{1,0:T(8,128)} fusion(bf16[2304,1536]{1,0:T(8,128)(2,1)} %fusion.40, bf16[2304,4608]{1,0:T(8,128)(2,1)} %attn_bwd.3), kind=kOutput, calls=%fused_computation.142 | convolution fusion | flops 32614907904 | bytes 56623104 | tf_op jit(solution)/shard_map/dot_general | solution.py:28
  1648.4 58.9 %fusion.46 = bf16[2304,1536]{1,0:T(8,128)(2,1)S(1)} fusion(bf16[6144,1536]{1,0:T(8,128)(2,1)} %all-gather.20.cloned.1.call-done, bf16[2304,1536]{1,0:T(8,128)(2,1)} %get-tuple-element.61, bf16[2304,6144]{1,0:T(8,128)(2,1)} %convolution_convert_fusion.2), kind=kOutput, calls=%fused_computation.88 | convolution fusion | flops 43638718464 | bytes 61341696 | tf_op jit(solution)/shard_map/dot_general | solution.py:20
  1713.5 108.7 %collective-permute-done.7 = bf16[2,3,192,1536]{3,2,1,0:T(8,128)(2,1)} collective-permute-done((bf16[2,3,192,1536]{3,2,1,0:T(8,128)(2,1)}, bf16[2,3,192,1536]{3,2,1,0:T(8,128)(2,1)}, u32[]{:S(2)}, u32[]{:S(2)}) %collective-permute-start.7) | collective-permute-done | bytes 3538976 | tf_op jit(solution)/shard_map/ppermute | solution.py:259
  1830.2 148.8 %reduce-scatter.9.cloned.1.call-done = f32[192,4608]{1,0:T(8,128)} async-done(((f32[1536,4608]{1,0:T(8,128)}), f32[192,4608]{1,0:T(8,128)}) %reduce-scatter.9.cloned.1.call-update) | async-done | bytes 3538960 | tf_op jit(solution)/shard_map/reduce_scatter | solution.py:245
  1979.0 5.5 broadcast_select_fusion.4
  1985.9 236.3 %reduce-scatter.23.cloned.1.call-done = f32[768,1536]{1,0:T(8,128)} async-done(((f32[6144,1536]{1,0:T(8,128)}), f32[768,1536]{1,0:T(8,128)}) %reduce-scatter.23.cloned.1.call-update) | async-done | bytes 4718608 | tf_op jit(solution)/shard_map/reduce_scatter | solution.py:245
  2222.2 220.9 %reduce-scatter.21.cloned.1.call-done = f32[768,1536]{1,0:T(8,128)} async-done(((f32[6144,1536]{1,0:T(8,128)}), f32[768,1536]{1,0:T(8,128)}) %reduce-scatter.21.cloned.1.call-update) | async-done | bytes 4718608 | tf_op jit(solution)/shard_map/reduce_scatter | solution.py:245
  2443.1 9.7 broadcast_select_fusion
  2454.1 261.2 %reduce-scatter.19.cloned.1.call-done = f32[192,6144]{1,0:T(8,128)} async-done(((f32[1536,6144]{1,0:T(8,128)}), f32[192,6144]{1,0:T(8,128)}) %reduce-scatter.19.cloned.1.call-update) | async-done | bytes 4718608 | tf_op jit(solution)/shard_map/reduce_scatter | solution.py:245
  2715.3 220.8 %reduce-scatter.17.cloned.1.call-done = f32[192,6144]{1,0:T(8,128)} async-done(((f32[1536,6144]{1,0:T(8,128)}), f32[192,6144]{1,0:T(8,128)}) %reduce-scatter.17.cloned.1.call-update) | async-done | bytes 4718608 | tf_op jit(solution)/shard_map/reduce_scatter | solution.py:245
  2936.1 8.7 broadcast_select_fusion.2
  2955.8 8.0 copy.18
  2963.8 8.5 maximum_bitcast_fusion.1
  2982.1 66.4 %collective-permute-done.5 = f32[192,6144]{1,0:T(8,128)} collective-permute-done((f32[192,6144]{1,0:T(8,128)}, f32[192,6144]{1,0:T(8,128)}, u32[]{:S(2)}, u32[]{:S(2)}) %collective-permute-start.5) | collective-permute-done | bytes 4718624 | tf_op jit(solution)/shard_map/ppermute | solution.py:252
  (136 shorter events, 95.2 us)
Async XLA Ops:
  7.2 265.6 %all-gather.8.cloned.1.call-start = ((), (), s32[]{:S(2)}) async-start(), calls=%async_computation.8 | async-start | bytes 31850496 | tf_op jit(solution)/shard_map/all_gather | solution.py:230
  7.9 398.5 %all-gather.10.cloned.1.call-start = ((), (), s32[]{:S(2)}) async-start(), calls=%async_computation.9 | async-start | bytes 5308416 | tf_op jit(solution)/shard_map/all_gather | solution.py:227
  9.1 20.5 collective-permute-start
  31.9 393.2 %all-gather.12.cloned.1.call-start = ((), (), s32[]{:S(2)}) async-start(), calls=%async_computation.10 | async-start | bytes 21233664 | tf_op jit(solution)/shard_map/all_gather | solution.py:227
  33.8 98.6 %collective-permute-start.1 = (bf16[192,6144]{1,0:T(8,128)(2,1)S(1)}, bf16[192,6144]{1,0:T(8,128)(2,1)S(1)}, u32[]{:S(2)}, u32[]{:S(2)}) collective-permute-start(bf16[192,6144]{1,0:T(8,128)(2,1)S(1)} %dynamic-slice_bitcast_fusion.1), channel_id=1, source_target_pairs={{0,4},{4,0},{1,5},{5,1},{2,6},{6,2},{3,7},{7,3}} | collective-permute-start | bytes 7077896 | tf_op jit(solution)/shard_map/ppermute | solution.py:223
  137.4 340.1 %all-gather.14.cloned.1.call-start = ((), (), s32[]{:S(2)}) async-start(), calls=%async_computation.11 | async-start | bytes 21233664 | tf_op jit(solution)/shard_map/all_gather | solution.py:227
  140.6 100.0 %collective-permute-start.2 = (bf16[768,1536]{1,0:T(8,128)(2,1)}, bf16[768,1536]{1,0:T(8,128)(2,1)S(1)}, u32[]{:S(2)}, u32[]{:S(2)}) collective-permute-start(bf16[768,1536]{1,0:T(8,128)(2,1)} %dynamic-slice_bitcast_fusion), channel_id=1, source_target_pairs={{0,4},{4,0},{1,5},{5,1},{2,6},{6,2},{3,7},{7,3}} | collective-permute-start | bytes 7077896 | tf_op jit(solution)/shard_map/ppermute | solution.py:223
  245.7 426.2 %all-gather.16.cloned.1.call-start = ((), (), s32[]{:S(2)}) async-start(), calls=%async_computation.12 | async-start | bytes 5308416 | tf_op jit(solution)/shard_map/all_gather | solution.py:227
  246.3 444.7 %all-gather.18.cloned.1.call-start = ((), (), s32[]{:S(2)}) async-start(), calls=%async_computation.13 | async-start | bytes 21233664 | tf_op jit(solution)/shard_map/all_gather | solution.py:227
  246.9 556.6 %all-gather.20.cloned.1.call-start = ((), (), s32[]{:S(2)}) async-start(), calls=%async_computation.14 | async-start | bytes 21233664 | tf_op jit(solution)/shard_map/all_gather | solution.py:227
  272.5 1553.9 %reduce-scatter.15.cloned.1.call-start = ((), (), s32[]{:S(2)}) async-start(), calls=%async_computation.18 | async-start | bytes 10616832 | tf_op jit(solution)/shard_map/reduce_scatter | solution.py:245
  403.5 3.0 copy-start
  425.1 52.4 %copy-start.10 = (f32[2304]{0:T(1024)}, f32[2304]{0:T(1024)S(1)}, u32[]{:S(2)}) copy-start(f32[2304]{0:T(1024)S(1)} %fusion.59) | copy-start | bytes 27652
  536.9 41.3 %copy-start.6 = (bf16[2304,1536]{1,0:T(8,128)(2,1)}, bf16[2304,1536]{1,0:T(8,128)(2,1)S(1)}, u32[]{:S(2)}) copy-start(bf16[2304,1536]{1,0:T(8,128)(2,1)S(1)} %get-tuple-element.59) | copy-start | bytes 21233668
  537.0 41.3 %copy-start.18 = (f32[2304]{0:T(1024)}, f32[2304]{0:T(1024)S(1)}, u32[]{:S(2)}) copy-start(f32[2304]{0:T(1024)S(1)} %get-tuple-element.58) | copy-start | bytes 27652
  537.0 41.3 %copy-start.12 = (f32[2304]{0:T(1024)}, f32[2304]{0:T(1024)S(1)}, u32[]{:S(2)}) copy-start(f32[2304]{0:T(1024)S(1)} %fusion.60) | copy-start | bytes 27652
  669.0 3.0 copy-start.2
  672.0 71.4 %slice-start.2 = ((s8[7077888]{0:T(1024)(128)(4,1)}), s8[2883584]{0:T(1024)(128)(4,1)S(1)}, s32[]{:S(2)}) async-start(s8[7077888]{0:T(1024)(128)(4,1)} %bitcast.80), calls=%async_computation.25 | async-start | bytes 5767168
  691.0 52.4 %copy-start.14 = (f32[2304]{0:T(1024)}, f32[2304]{0:T(1024)S(1)}, u32[]{:S(2)}) copy-start(f32[2304]{0:T(1024)S(1)} %fusion.61) | copy-start | bytes 27652
  691.1 52.3 %slice-start.3 = ((s8[7077888]{0:T(1024)(128)(4,1)}), s8[4194304]{0:T(1024)(128)(4,1)S(1)}, s32[]{:S(2)}) async-start(s8[7077888]{0:T(1024)(128)(4,1)} %bitcast.80), calls=%async_computation.26 | async-start | bytes 8388608
  803.5 86.7 %copy-start.15 = (f32[2304]{0:T(1024)S(1)}, f32[2304]{0:T(1024)}, u32[]{:S(2)}) copy-start(f32[2304]{0:T(1024)} %copy-done.14) | copy-start | bytes 27652
  944.0 61.5 %copy-start.21 = (f32[2304]{0:T(1024)S(1)}, f32[2304]{0:T(1024)}, u32[]{:S(2)}) copy-start(f32[2304]{0:T(1024)} %copy-done.20) | copy-start | bytes 27652
  1005.5 12.0 copy-start.3
  1014.7 2.9 copy-start.4
  1032.1 794.3 %reduce-scatter.13.cloned.1.call-start = ((), (), s32[]{:S(2)}) async-start(), calls=%async_computation.17 | async-start | bytes 10616832 | tf_op jit(solution)/shard_map/reduce_scatter | solution.py:245
  1048.8 75.6 %copy-start.13 = (f32[2304]{0:T(1024)S(1)}, f32[2304]{0:T(1024)}, u32[]{:S(2)}) copy-start(f32[2304]{0:T(1024)} %copy-done.12) | copy-start | bytes 27652
  1124.4 84.4 %slice-start = ((s8[7077888]{0:T(1024)(128)(4,1)}), s8[2883584]{0:T(1024)(128)(4,1)S(1)}, s32[]{:S(2)}) async-start(s8[7077888]{0:T(1024)(128)(4,1)} %bitcast.76), calls=%async_computation.23 | async-start | bytes 5767168
  1166.9 41.9 %copy-start.19 = (f32[2304]{0:T(1024)S(1)}, f32[2304]{0:T(1024)}, u32[]{:S(2)}) copy-start(f32[2304]{0:T(1024)} %copy-done.18) | copy-start | bytes 27652
  1166.9 41.9 %slice-start.1 = ((s8[7077888]{0:T(1024)(128)(4,1)}), s8[4194304]{0:T(1024)(128)(4,1)S(1)}, s32[]{:S(2)}) async-start(s8[7077888]{0:T(1024)(128)(4,1)} %bitcast.76), calls=%async_computation.24 | async-start | bytes 8388608
  1279.2 86.7 %copy-start.11 = (f32[2304]{0:T(1024)S(1)}, f32[2304]{0:T(1024)}, u32[]{:S(2)}) copy-start(f32[2304]{0:T(1024)} %copy-done.10) | copy-start | bytes 27652
  1419.8 61.6 %copy-start.17 = (f32[2304]{0:T(1024)S(1)}, f32[2304]{0:T(1024)}, u32[]{:S(2)}) copy-start(f32[2304]{0:T(1024)} %copy-done.16) | copy-start | bytes 27652
  1481.4 12.0 copy-start.1
  1490.5 2.9 copy-start.7
  1508.0 322.2 %reduce-scatter.11.cloned.1.call-start = ((), (), s32[]{:S(2)}) async-start(), calls=%async_computation.16 | async-start | bytes 31850496 | tf_op jit(solution)/shard_map/reduce_scatter | solution.py:245
  1508.6 470.4 %reduce-scatter.9.cloned.1.call-start = ((), (), s32[]{:S(2)}) async-start(), calls=%async_computation.15 | async-start | bytes 31850496 | tf_op jit(solution)/shard_map/reduce_scatter | solution.py:245
  1645.9 576.3 %reduce-scatter.23.cloned.1.call-start = ((), (), s32[]{:S(2)}) async-start(), calls=%async_computation.22 | async-start | bytes 42467328 | tf_op jit(solution)/shard_map/reduce_scatter | solution.py:245
  1646.4 796.7 %reduce-scatter.21.cloned.1.call-start = ((), (), s32[]{:S(2)}) async-start(), calls=%async_computation.21 | async-start | bytes 42467328 | tf_op jit(solution)/shard_map/reduce_scatter | solution.py:245
  1647.2 1068.1 %reduce-scatter.19.cloned.1.call-start = ((), (), s32[]{:S(2)}) async-start(), calls=%async_computation.20 | async-start | bytes 42467328 | tf_op jit(solution)/shard_map/reduce_scatter | solution.py:245
  1647.8 1288.3 %reduce-scatter.17.cloned.1.call-start = ((), (), s32[]{:S(2)}) async-start(), calls=%async_computation.19 | async-start | bytes 42467328 | tf_op jit(solution)/shard_map/reduce_scatter | solution.py:245
  1709.5 112.7 %collective-permute-start.7 = (bf16[2,3,192,1536]{3,2,1,0:T(8,128)(2,1)}, bf16[2,3,192,1536]{3,2,1,0:T(8,128)(2,1)}, u32[]{:S(2)}, u32[]{:S(2)}) collective-permute-start(bf16[2,3,192,1536]{3,2,1,0:T(8,128)(2,1)} %get-tuple-element.44), channel_id=1, source_target_pairs={{0,4},{4,0},{1,5},{5,1},{2,6},{6,2},{3,7},{7,3}} | collective-permute-start | bytes 10616840 | tf_op jit(solution)/shard_map/ppermute | solution.py:259
  1829.7 1116.9 %collective-permute-start.4 = (f32[192,1536]{1,0:T(8,128)}, f32[192,1536]{1,0:T(8,128)}, u32[]{:S(2)}, u32[]{:S(2)}) collective-permute-start(f32[192,1536]{1,0:T(8,128)} %get-tuple-element.52), channel_id=1, source_target_pairs={{0,4},{4,0},{1,5},{5,1},{2,6},{6,2},{3,7},{7,3}} | collective-permute-start | bytes 3538952 | tf_op jit(solution)/shard_map/ppermute | solution.py:252
  1984.4 967.3 %collective-permute-start.3 = (f32[192,4608]{1,0:T(8,128)}, f32[192,4608]{1,0:T(8,128)}, u32[]{:S(2)}, u32[]{:S(2)}) collective-permute-start(f32[192,4608]{1,0:T(8,128)} %get-tuple-element.46), channel_id=1, source_target_pairs={{0,4},{4,0},{1,5},{5,1},{2,6},{6,2},{3,7},{7,3}} | collective-permute-start | bytes 10616840 | tf_op jit(solution)/shard_map/ppermute | solution.py:252
  2452.8 524.4 %collective-permute-start.6 = (f32[768,1536]{1,0:T(8,128)}, f32[768,1536]{1,0:T(8,128)}, u32[]{:S(2)}, u32[]{:S(2)}) collective-permute-start(f32[768,1536]{1,0:T(8,128)} %get-tuple-element.40), channel_id=1, source_target_pairs={{0,4},{4,0},{1,5},{5,1},{2,6},{6,2},{3,7},{7,3}} | collective-permute-start | bytes 14155784 | tf_op jit(solution)/shard_map/ppermute | solution.py:252
  2936.1 10.2 copy-start.8
  2944.8 103.7 %collective-permute-start.5 = (f32[192,6144]{1,0:T(8,128)}, f32[192,6144]{1,0:T(8,128)}, u32[]{:S(2)}, u32[]{:S(2)}) collective-permute-start(f32[192,6144]{1,0:T(8,128)} %get-tuple-element.42), channel_id=1, source_target_pairs={{0,4},{4,0},{1,5},{5,1},{2,6},{6,2},{3,7},{7,3}} | collective-permute-start | bytes 14155784 | tf_op jit(solution)/shard_map/ppermute | solution.py:252
  2948.0 3.8 copy-start.9
  2955.8 16.6 slice-start.4
  2963.8 8.5 slice-start.5
  (3 other events, 4.0 us)
Sparse Core Ops, SparseCore 0:
  9.8 237.3 all-gather.7
  249.6 34.5 all-gather.9
  285.9 93.1 all-gather.11
  380.8 93.0 all-gather.13
  475.5 33.2 all-gather.15
  510.5 93.0 all-gather.17
  605.9 93.2 all-gather.19
  1032.2 69.4 reduce-scatter.14
  1508.1 69.5 reduce-scatter.12
  1581.1 201.7 reduce-scatter.10
  1786.6 192.3 reduce-scatter.8
  1982.4 239.7 reduce-scatter.22
  2225.7 217.3 reduce-scatter.20
  2446.5 268.6 reduce-scatter.18
  2718.7 217.3 reduce-scatter.16
